TPU v7x, 32 devices: a whole 2x2x4 slice. The times are simulated.
32 devices in a mesh: rows: 8 (over z, y), rhs: 4 (over x, core).
Axes of the slice: x: 2, y: 2, z: 4, core: 2. Of those that a mesh axis runs over, the one named last changes fastest.
Arguments:
- right_sides: bfloat16 [64, 16384], P('rhs', 'rows'), may hold values from -6 to 6
- lower_inverse: bfloat16 [64, 256, 256], P('rows'), may hold values from -0.375 to 0.375
- lower_left: bfloat16 [64, 256, 32], P('rows'), may hold values from -1 to 1
- lower_right: bfloat16 [64, 256, 32], P('rows'), may hold values from -0.015625 to 0.015625
- upper_inverse: bfloat16 [64, 256, 256], P('rows'), may hold values from -0.375 to 0.375
- upper_left: bfloat16 [64, 256, 32], P('rows'), may hold values from -1 to 1
- upper_right: bfloat16 [64, 256, 32], P('rows'), may hold values from -0.015625 to 0.015625
- block_ranks: int32 [2, 64], P(None, 'rows'), may hold values from 8 to 32
Outputs:
- first_solve: float32 [64, 16384], P('rhs', 'rows')
- second_solve: float32 [64, 16384], P('rhs', 'rows')
All inputs are finite; a program needn't handle non-finite values.
Results may differ from a plain program's by a relative error of at most 0.0051.
Values may be sent and summed in bfloat16 or wider, within the bound.
A program may use at most 64 MiB of HBM per device.

v0:
```python
import functools

import jax
import jax.numpy as jnp
from jax import lax
from jax.experimental import pallas as pl
from jax.experimental.pallas import tpu as pltpu
from jax.sharding import PartitionSpec as P

MESH = pl.DeviceIdType.MESH
LANES = 128
f32, bf16 = jnp.float32, jnp.bfloat16


def split(x):
    hi = x.astype(bf16)
    return hi, (x - hi.astype(f32)).astype(bf16)


def dot(a, b):
    return jnp.dot(a, b, preferred_element_type=f32)


def dot_nt(a, b):
    return lax.dot_general(a, b, (((1,), (1,)), ((), ())), preferred_element_type=f32)


def dot_split(a, b_hi, b_lo):
    a_hi, a_lo = split(a)
    rows = a.shape[0]
    both = dot(jnp.concatenate([a_hi, a_lo], axis=0), b_hi)
    return both[:rows] + both[rows:] + dot(a_hi, b_lo)


def dot_full(a, b):
    return dot_split(a, *split(b))


def grow(x, rows):
    if x.shape[0] == rows:
        return x
    return jnp.concatenate([x, jnp.zeros((rows - x.shape[0], LANES), f32)], axis=0)


def each(count, body):
    if count <= 8:
        for i in range(count):
            body(i)
    else:
        lax.fori_loop(0, count, lambda i, c: (body(i), c)[1], 0)


def kernel(
    R, nb, bs, w, n,
    rhs_h, linv_h, llt_h, lrt_h, uinv_h, ult_h, urt_h, ranks_h,
    first, second,
    rhs, llt, lrt, ult, urt, ranks,
    inv, ctp, ntp, wst, hs, got0, got1, got2, send0, send1, send2, g, walk, table, y,
    load_sem, block_sem, send_sem, recv_sem,
):
    me = lax.axis_index("rows")
    group = LANES // w
    quads = nb // group
    half = n // 2

    small = [
        pltpu.make_async_copy(src, dst, load_sem.at[i])
        for i, (src, dst) in enumerate(
            ((llt_h, llt), (lrt_h, lrt), (ranks_h, ranks), (ult_h, ult), (urt_h, urt), (rhs_h, rhs))
        )
    ]
    large = [
        [
            pltpu.make_async_copy(src.at[b], inv.at[f, b], block_sem.at[f, b])
            for b in (range(nb) if f == 0 else reversed(range(nb)))
        ]
        for f, src in ((0, linv_h), (1, uinv_h))
    ]
    for cp in small[:3] + large[0] + small[3:5] + large[1] + small[5:]:
        cp.start()

    barrier = pltpu.get_barrier_semaphore()

    def greet(i):
        pl.semaphore_signal(
            barrier, inc=1, device_id={"rows": lax.rem(me + i + 1, R)}, device_id_type=MESH
        )

    each(R - 1, greet)

    ctp[...] = jnp.zeros_like(ctp)
    ntp[...] = jnp.zeros_like(ntp)

    lane = lax.broadcasted_iota(jnp.int32, (w, LANES), 1)
    row = lax.broadcasted_iota(jnp.int32, (w, LANES), 0)
    eye = (lax.rem(lane, w) == row).astype(f32)

    def lanes(rows):
        return lax.broadcasted_iota(jnp.int32, (rows, LANES), 1)

    def block(f, p):
        return p if f == 0 else nb - 1 - p

    lefts, rights = (llt, ult), (lrt, urt)
    kernels = ([], [])
    maps = [None, None]
    for f in (0, 1):
        for cp in small[:3] if f == 0 else small[3:5]:
            cp.wait()
        wide_row = lax.broadcasted_iota(jnp.int32, (w, bs), 0)
        for p in range(nb):
            b = block(f, p)
            large[f][p].wait()
            at = pl.ds(w * (p % group), w)
            ct = dot_nt(lefts[f][b], inv[f, b]).astype(bf16)
            ctp[f, p, at, :] = ct
            mt = jnp.where(wide_row < ranks[f, b], rights[f][b].astype(f32), 0.0).astype(bf16)
            hi, lo = split(dot(mt, inv[f, b]))
            ntp[f, 0, p, at, :] = hi
            ntp[f, 1, p, at, :] = lo
            kernels[f].append(eye - dot_nt(ct, jnp.concatenate([mt] * group, axis=0)))

    chains = {}
    for q in range(quads):
        for f in (0, 1):
            chains[f, q] = [eye]
    for k in range(group):
        for q in range(quads):
            for f in (0, 1):
                last = chains[f, q][-1]
                moved = dot_full(last[:, :w], kernels[f][q * group + k])
                chains[f, q].append(jnp.concatenate([moved, eye], axis=0))

    full = w * (nb + 1)
    joined = {}
    for f in (0, 1):
        before = None
        for q in range(quads):
            grown = w * (group + 1)
            total = jnp.zeros((grown, LANES), f32)
            for k in range(group):
                col = chains[f, q][k]
                total = jnp.where(lanes(grown) // w == k, grow(col, grown), total)
            end = chains[f, q][group]
            if before is not None:
                moved = dot_full(before[:, :w], jnp.concatenate([total[:w], end[:w]], axis=1))
                total = jnp.concatenate([moved[:, :LANES], total[w:]], axis=0)
                end = jnp.concatenate([moved[:, LANES:], end[w:]], axis=0)
            joined[f, q] = grow(total, full)
            before = end
        maps[f] = before[:w]
        hi, lo = split(before[w:])
        wst[f, 0, quads] = hi
        wst[f, 1, quads] = lo

    narrow = w // group
    narrow_lanes = lanes(narrow) // w

    def fold_map(x):
        out = x[:narrow]
        for k in range(1, group):
            out = jnp.where(narrow_lanes == k, x[k * narrow : (k + 1) * narrow], out)
        return out

    def tile(x):
        return jnp.concatenate([x] * group, axis=0)

    def expand(x):
        return jnp.where(lane // w == row // narrow, tile(x), 0.0)

    def copy(k, src, dst, i):
        peer = lax.rem(me + i + 1, R)
        return pltpu.make_async_remote_copy(
            src_ref=src, dst_ref=dst.at[me], send_sem=send_sem.at[k, i],
            recv_sem=recv_sem.at[k, me], device_id={"rows": peer}, device_id_type=MESH,
        )

    def arrive(k, src, dst, i):
        peer = lax.rem(me + i + 1, R)
        pltpu.make_async_remote_copy(
            src_ref=src, dst_ref=dst.at[peer], send_sem=send_sem.at[k, i],
            recv_sem=recv_sem.at[k, peer], device_id={"rows": peer}, device_id_type=MESH,
        ).wait_recv()

    send0[:narrow] = fold_map(maps[0])
    send0[narrow:] = fold_map(maps[1])
    pl.semaphore_wait(barrier, R - 1)
    each(R - 1, lambda i: copy(0, send0, got0, i).start())
    got0[me] = send0[...]

    for f in (0, 1):
        for q in range(quads):
            total = joined[f, q]
            hi, lo = split(total[w:])
            wst[f, 0, q] = hi
            wst[f, 1, q] = lo
            p_hi, p_lo = split(total[:w])
            lhs = jnp.concatenate([p_hi, p_lo], axis=0)
            for k in range(group):
                p = q * group + k
                b = block(f, p)
                both = dot(lhs, ctp[f, p])
                hi, lo = split(both[:w] + both[w:])
                hs[f, :, b * bs : (b + 1) * bs] = jnp.concatenate([hi, hi, lo, lo], axis=0)

    def pushes(f, piece):
        parts = []
        for q in range(quads):
            total = None
            for k in range(group):
                p = q * group + k
                v = piece(block(f, p))
                term = dot_nt(v, ntp[f, 0, p]) + dot_nt(v, ntp[f, 1, p])
                total = term if total is None else total + term
            parts.append(total)
        return jnp.concatenate(parts, axis=1)

    def message(f, u):
        return dot_split(u, wst[f, 0, quads], wst[f, 1, quads])

    def local_blocks(f, piece, u):
        out = {}
        for q in range(quads):
            x_hi, x_lo = split(dot_split(u, wst[f, 0, q], wst[f, 1, q]))
            lhs = jnp.concatenate([x_hi, x_lo], axis=0)
            for k in range(group):
                p = q * group + k
                b = block(f, p)
                both = dot(lhs, ctp[f, p])
                out[b] = dot_nt(piece(b), inv[f, b]) - both[:n] - both[n:]
        return out

    def cols(b):
        return slice(b * bs, (b + 1) * bs)

    def fold(m, z):
        mixed = jnp.where(lax.rem(lanes(n) // w, 2) == 0, m, z)
        return jnp.where(lanes(half) < LANES // 2, mixed[:half], mixed[half:])

    def unfold(x):
        low = lanes(half) < LANES // 2
        return jnp.concatenate([jnp.where(low, x, 0.0), jnp.where(low, 0.0, x)], axis=0)

    def sweep_start(piece):
        u = pushes(0, piece)
        m = message(0, u)
        out = local_blocks(0, piece, u)
        for b in range(nb):
            y[:, cols(b)] = out[b]
        return m

    def incoming(arrived):
        a = jnp.concatenate([unfold(arrived(e)) for e in range(R)], axis=1)
        a_hi, a_lo = split(a)
        both = jnp.concatenate([a_hi, a_lo], axis=0)
        states = []
        for k in (0, 1):
            r = dot(both, table[k, 0])
            s_hi, s_lo = split(r[:n] + r[n:] + dot(a_hi, table[k, 1]))
            even = lax.rem(lanes(n) // w, 2) == 0
            states.append(jnp.where(even, s_hi.astype(f32), s_lo.astype(f32)).astype(bf16))
        return states

    def sweep_end(s_f, s_b, out_ref):
        forward = [
            (y[:, cols(b)] - dot(s_f, hs[0, :, cols(b)])).astype(bf16) for b in range(nb)
        ]
        piece = lambda b: forward[b]
        u = pushes(1, piece)
        out = local_blocks(1, piece, u)
        for b in range(nb):
            out_ref[:, cols(b)] = out[b] - dot(s_b, hs[1, :, cols(b)])

    small[5].wait()
    m = sweep_start(lambda b: rhs[:, cols(b)])
    mixed = pushes(
        1,
        lambda b: jnp.concatenate(
            [*split(y[:, cols(b)]), hs[0, :w, cols(b)], hs[0, 2 * w : 3 * w, cols(b)]], axis=0
        ),
    )
    u = jnp.concatenate(
        [mixed[:n] + mixed[n : 2 * n], mixed[2 * n : 2 * n + w] + mixed[2 * n + w :]], axis=0
    )
    zm = message(1, u)
    send1[:narrow] = fold_map(zm[n:])
    send1[narrow:] = fold(m, zm[:n])
    each(R - 1, lambda i: copy(1, send1, got1, i).start())
    got1[me] = send1[...]

    zero = jnp.zeros((w, LANES), f32)
    spot = jnp.where(lane < w, eye, 0.0)
    each(R - 1, lambda i: arrive(0, send0, got0, i))
    g[1, 0:w] = zero

    def rows_of(d):
        return pl.ds(d * w if isinstance(d, int) else pl.multiple_of(d * w, w), w)

    def backward_map(d):
        moved = dot_full(expand(got0[d, narrow:]), tile(g[1, rows_of(d)]))
        g[1, rows_of(d + 1)] = moved + jnp.where(me == d, eye, 0.0)

    def forward_map(d, state):
        return dot_full(state, tile(expand(got0[d, :narrow])))

    def crossed(d, state):
        return dot_full(
            dot_full(state, tile(expand(got1[d, :narrow]))), tile(g[1, rows_of(d)])
        )

    if R <= 8:
        history = [None]
        for d in range(R - 1):
            backward_map(d)
            last = history[-1]
            grown = spot if last is None else jnp.concatenate([forward_map(d, last), spot], axis=0)
            history.append(grown)
        chosen = jnp.zeros((R * w, LANES), f32)
        for d in range(1, R):
            chosen = jnp.where(me == d, grow(history[d], R * w), chosen)
        g[0] = chosen
        each(R - 1, lambda i: arrive(1, send1, got1, i))
        total = jnp.zeros((R * w, LANES), f32)
        for d in range(1, R):
            total += grow(crossed(d, history[d]), R * w)
        g[2] = total
    else:
        each(R - 1, backward_map)
        each(R - 1, lambda i: arrive(1, send1, got1, i))
        walk[...] = jnp.zeros_like(walk)
        g[0] = jnp.zeros((R * w, LANES), f32)
        g[2] = jnp.zeros((R * w, LANES), f32)

        def step(d):
            state = walk[...]
            g[0] = jnp.where(me == d, state, g[0])
            g[2] = g[2] + crossed(d, state)
            walk[...] = forward_map(d, state)
            walk[rows_of(d)] = spot

        each(R, step)

    c_hi, c_lo = split(g[0])
    spread = tile(eye).astype(bf16)
    g[0] = dot(c_hi, spread) + dot(c_lo, spread)

    def fill(e):
        at = pl.ds(e * LANES if isinstance(e, int) else pl.multiple_of(e * LANES, LANES), LANES)
        hi, lo = split(jnp.concatenate([g[0, rows_of(e)], zero] * 2, axis=0))
        table[0, 0, at] = hi
        table[0, 1, at] = lo
        hi, lo = split(jnp.concatenate([-g[2, rows_of(e)], g[1, rows_of(e)]] * 2, axis=0))
        table[1, 0, at] = hi
        table[1, 1, at] = lo

    each(R, fill)

    s_f, s_b = incoming(lambda e: got1[e, narrow:])
    sweep_end(s_f, s_b, first)

    m = sweep_start(lambda b: first[:, cols(b)].astype(bf16))
    mixed = pushes(1, lambda b: jnp.concatenate(split(y[:, cols(b)]), axis=0))
    z = message(1, mixed[:n] + mixed[n:])
    send2[...] = fold(m, z)
    each(R - 1, lambda i: copy(2, send2, got2, i).start())
    got2[me] = send2[...]
    each(R - 1, lambda i: arrive(2, send2, got2, i))
    s_f, s_b = incoming(lambda e: got2[e])
    sweep_end(s_f, s_b, second)

    each(R - 1, lambda i: copy(0, send0, got0, i).wait_send())
    each(R - 1, lambda i: copy(1, send1, got1, i).wait_send())
    each(R - 1, lambda i: copy(2, send2, got2, i).wait_send())


def local(R, rhs, linv, lleft, lright, uinv, uleft, uright, ranks):
    nb, bs, w = lleft.shape
    n = rhs.shape[0]
    flip = lambda a: jnp.swapaxes(a, 1, 2)
    vmem = pl.BlockSpec(memory_space=pltpu.VMEM)
    hbm = pl.BlockSpec(memory_space=pltpu.HBM)
    quads = nb * w // LANES
    out = jax.ShapeDtypeStruct(rhs.shape, f32)
    narrow = w * w // LANES
    packed = narrow + n // 2
    slim = pltpu.VMEM((nb, w, bs), bf16)
    return pl.pallas_call(
        functools.partial(kernel, R, nb, bs, w, n),
        out_shape=(out, out),
        in_specs=[hbm] * 8,
        out_specs=(vmem, vmem),
        scratch_shapes=[
            pltpu.VMEM(rhs.shape, bf16),
            slim, slim, slim, slim,
            pltpu.SMEM(ranks.shape, jnp.int32),
            pltpu.VMEM((2, nb, bs, bs), bf16),
            pltpu.VMEM((2, nb, LANES, bs), bf16),
            pltpu.VMEM((2, 2, nb, LANES, bs), bf16),
            pltpu.VMEM((2, 2, quads + 1, nb * w, LANES), bf16),
            pltpu.VMEM((2, 4 * w, nb * bs), bf16),
            pltpu.VMEM((R, 2 * narrow, LANES), f32),
            pltpu.VMEM((R, packed, LANES), f32),
            pltpu.VMEM((R, n // 2, LANES), f32),
            pltpu.VMEM((2 * narrow, LANES), f32),
            pltpu.VMEM((packed, LANES), f32),
            pltpu.VMEM((n // 2, LANES), f32),
            pltpu.VMEM((3, R * w, LANES), f32),
            pltpu.VMEM((R * w, LANES), f32),
            pltpu.VMEM((2, 2, R * LANES, LANES), bf16),
            pltpu.VMEM((n, nb * bs), f32),
            pltpu.SemaphoreType.DMA((6,)),
            pltpu.SemaphoreType.DMA((2, nb)),
            pltpu.SemaphoreType.DMA((3, R)),
            pltpu.SemaphoreType.DMA((3, R)),
        ],
        compiler_params=pltpu.CompilerParams(
            collective_id=0, has_side_effects=True, vmem_limit_bytes=67043328
        ),
    )(rhs, linv, flip(lleft), flip(lright), uinv, flip(uleft), flip(uright), ranks)


def solution(mesh):
    blocks = P("rows", None, None)
    placed = (P("rhs", "rows"),) + (blocks,) * 6 + (P(None, "rows"),)
    return jax.shard_map(
        functools.partial(local, mesh.shape["rows"]),
        mesh=mesh,
        in_specs=placed,
        out_specs=(P("rhs", "rows"), P("rhs", "rows")),
        check_vma=False,
    )
```

profile of v0, /device:TPU:0, one launch (start us, length us, event | category | flops | bytes accessed | tf_op | source)
XLA Modules:
  0.0 28.7 jit_solution(11492553986708118739)
XLA Ops:
  0.6 25.7 %shard_map.95 = (f32[16,2048]{1,0:T(8,128)}, f32[16,2048]{1,0:T(8,128)}) custom-call(bf16[16,2048]{1,0:T(8,128)(2,1)} %rhs_h.1, bf16[8,256,256]{2,1,0:T(8,128)(2,1)} %linv_h.1, bf16[8,32,256]{2,1,0:T(8,128)(2,1)} %bitcast.4, bf16[8,32,256]{2,1,0:T(8,128)(2,1)} %bitcast.5, bf16[8,256,256]{2,1,0:T(8,128)(2,1)} %uinv_h.1, bf16[8,32,256]{2,1,0:T(8,128)(2,1)} %bitcast.6, ...), custom_call_target="tpu_custom_call" | custom-call | tf_op jit(solution)/shard_map/pallas_call | solution.py:387
  26.4 0.0 copy-start
  26.4 1.6 %copy.12 = f32[16,2048]{1,0:T(8,128)} copy(f32[16,2048]{1,0:T(8,128)} %get-tuple-element.4) | data formatting | bytes 262144
  28.0 0.0 copy-done
  28.0 0.7 %copy.13 = f32[16,2048]{1,0:T(8,128)} copy(f32[16,2048]{1,0:T(8,128)S(1)} %copy-done) | data formatting | bytes 262144
Async XLA Ops:
  26.4 1.6 %copy-start = (f32[16,2048]{1,0:T(8,128)S(1)}, f32[16,2048]{1,0:T(8,128)}, u32[]{:S(2)}) copy-start(f32[16,2048]{1,0:T(8,128)} %get-tuple-element.5) | copy-start | bytes 393220
where the time goes:
time: 28.8 us; the launch traced here: 28.7 us
  Pallas kernels  25.7 us (89%)
  local copies, waits for them, and re-layouts  2.26 us (8%)
  between operations  0.65 us (2%)
    pallas_call x1, Pallas kernels, local(): pl.pallas_call(functools.partial(kernel, R, nb, bs, w, n), out_shape=(out...  25.7 us
    unnamed x4, local copies, waits for them, and re-layouts  2.26 us

commit v1 on v0

--- a/solution.py
+++ b/solution.py
@@ -414,7 +414,7 @@
             pltpu.SemaphoreType.DMA((3, R)),
         ],
         compiler_params=pltpu.CompilerParams(
-            collective_id=0, has_side_effects=True, vmem_limit_bytes=67043328
+            collective_id=0, has_side_effects=True, vmem_limit_bytes=33554432
         ),
     )(rhs, linv, flip(lleft), flip(lright), uinv, flip(uleft), flip(uright), ranks)
 

time: 28.8 us -> 36.9 us (1.28)
  local copies, waits for them, and re-layouts: 2.26 us -> 8.89 us
  Pallas kernels: 25.7 us -> 27.1 us
    unnamed x4 -> x18, local copies, waits for them, and re-layouts: 2.26 us -> 8.89 us
    pallas_call x1, Pallas kernels: 25.7 us -> 27.1 us  [local(): pl.pallas_call(functools.partial(kernel, R, nb, bs, w, n), out_shape=(out...]
where the time goes in v1:
time: 36.9 us; the launch traced here: 36.6 us
  Pallas kernels  27.1 us (73%)
  local copies, waits for them, and re-layouts  8.89 us (24%)
  between operations  0.66 us (2%)
    pallas_call x1, Pallas kernels, local(): pl.pallas_call(functools.partial(kernel, R, nb, bs, w, n), out_shape=(out...  27.1 us
    unnamed x18, local copies, waits for them, and re-layouts  8.89 us

profile of v1, /device:TPU:0, one launch (start us, length us, event | category | flops | bytes accessed | tf_op | source)
XLA Modules:
  0.0 36.6 jit_solution(2239149900647865999)
XLA Ops:
  0.6 0.0 copy-start.7
  0.6 0.7 %copy-done.7 = s32[2,8]{1,0:T(2,128)S(1)} copy-done((s32[2,8]{1,0:T(2,128)S(1)}, s32[2,8]{1,0:T(2,128)}, u32[]{:S(2)}) %copy-start.7) | copy-done | bytes 88
  1.3 0.0 copy-start
  1.3 1.2 %copy-done = bf16[8,256,256]{2,1,0:T(8,128)(2,1)S(1)} copy-done((bf16[8,256,256]{2,1,0:T(8,128)(2,1)S(1)}, bf16[8,256,256]{2,1,0:T(8,128)(2,1)}, u32[]{:S(2)}) %copy-start) | copy-done | bytes 1048600
  2.5 0.0 copy-start.1
  2.5 1.2 %copy-done.1 = bf16[8,256,256]{2,1,0:T(8,128)(2,1)S(1)} copy-done((bf16[8,256,256]{2,1,0:T(8,128)(2,1)S(1)}, bf16[8,256,256]{2,1,0:T(8,128)(2,1)}, u32[]{:S(2)}) %copy-start.1) | copy-done | bytes 1048600
  3.8 0.0 copy-start.2
  3.8 0.9 %copy-done.2 = bf16[8,256,32]{1,2,0:T(8,128)(2,1)S(1)} copy-done((bf16[8,256,32]{1,2,0:T(8,128)(2,1)S(1)}, bf16[8,256,32]{1,2,0:T(8,128)(2,1)}, u32[]{:S(2)}) %copy-start.2) | copy-done | bytes 131096
  4.7 0.0 copy-start.3
  4.7 0.9 %copy-done.3 = bf16[8,256,32]{1,2,0:T(8,128)(2,1)S(1)} copy-done((bf16[8,256,32]{1,2,0:T(8,128)(2,1)S(1)}, bf16[8,256,32]{1,2,0:T(8,128)(2,1)}, u32[]{:S(2)}) %copy-start.3) | copy-done | bytes 131096
  5.6 0.0 copy-start.4
  5.6 0.9 %copy-done.4 = bf16[8,256,32]{1,2,0:T(8,128)(2,1)S(1)} copy-done((bf16[8,256,32]{1,2,0:T(8,128)(2,1)S(1)}, bf16[8,256,32]{1,2,0:T(8,128)(2,1)}, u32[]{:S(2)}) %copy-start.4) | copy-done | bytes 131096
  6.5 0.0 copy-start.5
  6.5 0.9 %copy-done.5 = bf16[8,256,32]{1,2,0:T(8,128)(2,1)S(1)} copy-done((bf16[8,256,32]{1,2,0:T(8,128)(2,1)S(1)}, bf16[8,256,32]{1,2,0:T(8,128)(2,1)}, u32[]{:S(2)}) %copy-start.5) | copy-done | bytes 131096
  7.4 0.0 copy-start.6
  7.4 0.8 %copy-done.6 = bf16[16,2048]{1,0:T(8,128)(2,1)S(1)} copy-done((bf16[16,2048]{1,0:T(8,128)(2,1)S(1)}, bf16[16,2048]{1,0:T(8,128)(2,1)}, u32[]{:S(2)}) %copy-start.6) | copy-done | bytes 65560
  8.2 27.1 %shard_map.95 = (f32[16,2048]{1,0:T(8,128)S(1)}, f32[16,2048]{1,0:T(8,128)S(1)}) custom-call(bf16[16,2048]{1,0:T(8,128)(2,1)S(1)} %copy-done.6, bf16[8,256,256]{2,1,0:T(8,128)(2,1)S(1)} %copy-done, bf16[8,32,256]{2,1,0:T(8,128)(2,1)S(1)} %bitcast.4, bf16[8,32,256]{2,1,0:T(8,128)(2,1)S(1)} %bitcast.5, bf16[8,256,256]{2,1,0:T(8,128)(2,1)S(1)} %copy-done.1, ...), custom_call_target="tpu_custom_call" | custom-call | tf_op jit(solution)/shard_map/pallas_call | solution.py:387
  35.3 0.7 %copy.12 = f32[16,2048]{1,0:T(8,128)} copy(f32[16,2048]{1,0:T(8,128)S(1)} %get-tuple-element.4) | data formatting | bytes 262144
  35.9 0.7 %copy.13 = f32[16,2048]{1,0:T(8,128)} copy(f32[16,2048]{1,0:T(8,128)S(1)} %get-tuple-element.5) | data formatting | bytes 262144
Async XLA Ops:
  0.6 0.7 %copy-start.7 = (s32[2,8]{1,0:T(2,128)S(1)}, s32[2,8]{1,0:T(2,128)}, u32[]{:S(2)}) copy-start(s32[2,8]{1,0:T(2,128)} %ranks_h.1) | copy-start | bytes 196
  1.3 1.2 %copy-start = (bf16[8,256,256]{2,1,0:T(8,128)(2,1)S(1)}, bf16[8,256,256]{2,1,0:T(8,128)(2,1)}, u32[]{:S(2)}) copy-start(bf16[8,256,256]{2,1,0:T(8,128)(2,1)} %linv_h.1) | copy-start | bytes 3145732
  2.5 1.2 %copy-start.1 = (bf16[8,256,256]{2,1,0:T(8,128)(2,1)S(1)}, bf16[8,256,256]{2,1,0:T(8,128)(2,1)}, u32[]{:S(2)}) copy-start(bf16[8,256,256]{2,1,0:T(8,128)(2,1)} %uinv_h.1) | copy-start | bytes 3145732
  3.8 0.9 %copy-start.2 = (bf16[8,256,32]{1,2,0:T(8,128)(2,1)S(1)}, bf16[8,256,32]{1,2,0:T(8,128)(2,1)}, u32[]{:S(2)}) copy-start(bf16[8,256,32]{1,2,0:T(8,128)(2,1)} %param.10) | copy-start | bytes 393220
  4.7 0.9 %copy-start.3 = (bf16[8,256,32]{1,2,0:T(8,128)(2,1)S(1)}, bf16[8,256,32]{1,2,0:T(8,128)(2,1)}, u32[]{:S(2)}) copy-start(bf16[8,256,32]{1,2,0:T(8,128)(2,1)} %param.11) | copy-start | bytes 393220
  5.6 0.9 %copy-start.4 = (bf16[8,256,32]{1,2,0:T(8,128)(2,1)S(1)}, bf16[8,256,32]{1,2,0:T(8,128)(2,1)}, u32[]{:S(2)}) copy-start(bf16[8,256,32]{1,2,0:T(8,128)(2,1)} %param.13) | copy-start | bytes 393220
  6.5 0.9 %copy-start.5 = (bf16[8,256,32]{1,2,0:T(8,128)(2,1)S(1)}, bf16[8,256,32]{1,2,0:T(8,128)(2,1)}, u32[]{:S(2)}) copy-start(bf16[8,256,32]{1,2,0:T(8,128)(2,1)} %param.14) | copy-start | bytes 393220
  7.4 0.8 %copy-start.6 = (bf16[16,2048]{1,0:T(8,128)(2,1)S(1)}, bf16[16,2048]{1,0:T(8,128)(2,1)}, u32[]{:S(2)}) copy-start(bf16[16,2048]{1,0:T(8,128)(2,1)} %rhs_h.1) | copy-start | bytes 196612

commit v2 on v1

--- a/solution.py
+++ b/solution.py
@@ -416,7 +416,7 @@
         compiler_params=pltpu.CompilerParams(
             collective_id=0, has_side_effects=True, vmem_limit_bytes=33554432
         ),
-    )(rhs, linv, flip(lleft), flip(lright), uinv, flip(uleft), flip(uright), ranks)
+    )(*[pltpu.with_memory_space_constraint(a, pltpu.HBM) for a in (rhs, linv, flip(lleft), flip(lright), uinv, flip(uleft), flip(uright), ranks)])
 
 
 def solution(mesh):

time: 36.9 us -> 27.2 us (0.74)
  local copies, waits for them, and re-layouts: 8.89 us -> 1.31 us
  Pallas kernels: 27.1 us -> 25.1 us
    unnamed x18 -> x2, local copies, waits for them, and re-layouts: 8.89 us -> 1.31 us
    pallas_call x1, Pallas kernels: 27.1 us -> 25.1 us  [local(): pl.pallas_call(functools.partial(kernel, R, nb, bs, w, n), out_shape=(out...]
where the time goes in v2:
time: 27.2 us; the launch traced here: 27 us
  Pallas kernels  25.1 us (92%)
  local copies, waits for them, and re-layouts  1.31 us (5%)
  between operations  0.64 us (2%)
    pallas_call x1, Pallas kernels, local(): pl.pallas_call(functools.partial(kernel, R, nb, bs, w, n), out_shape=(out...  25.1 us
    unnamed x2, local copies, waits for them, and re-layouts  1.31 us

profile of v2, /device:TPU:0, one launch (start us, length us, event | category | flops | bytes accessed | tf_op | source)
XLA Modules:
  0.0 27.0 jit_solution(7730145836462747961)
XLA Ops:
  0.6 25.1 %shard_map.95 = (f32[16,2048]{1,0:T(8,128)S(1)}, f32[16,2048]{1,0:T(8,128)S(1)}) custom-call(bf16[16,2048]{1,0:T(8,128)(2,1)} %rhs_h.1, bf16[8,256,256]{2,1,0:T(8,128)(2,1)} %linv_h.1, bf16[8,32,256]{2,1,0:T(8,128)(2,1)} %bitcast.4, bf16[8,32,256]{2,1,0:T(8,128)(2,1)} %bitcast.5, bf16[8,256,256]{2,1,0:T(8,128)(2,1)} %uinv_h.1, bf16[8,32,256]{2,1,0:T(8,128)(2,1)} %bitcast.6, ...), custom_call_target="tpu_custom_call" | custom-call | tf_op jit(solution)/shard_map/pallas_call | solution.py:387
  25.7 0.7 %copy.12 = f32[16,2048]{1,0:T(8,128)} copy(f32[16,2048]{1,0:T(8,128)S(1)} %get-tuple-element.4) | data formatting | bytes 262144
  26.4 0.7 %copy.13 = f32[16,2048]{1,0:T(8,128)} copy(f32[16,2048]{1,0:T(8,128)S(1)} %get-tuple-element.5) | data formatting | bytes 262144

commit v3 on v2

v3 whole, which is shorter than its diff:
```python
import functools

import jax
import jax.numpy as jnp
from jax import lax
from jax.experimental import pallas as pl
from jax.experimental.pallas import tpu as pltpu
from jax.sharding import PartitionSpec as P

MESH = pl.DeviceIdType.MESH
LANES = 128
f32, bf16 = jnp.float32, jnp.bfloat16


def split(x):
    hi = x.astype(bf16)
    return hi, (x - hi.astype(f32)).astype(bf16)


def dot(a, b):
    return jnp.dot(a, b, preferred_element_type=f32)


def dot_nt(a, b):
    return lax.dot_general(a, b, (((1,), (1,)), ((), ())), preferred_element_type=f32)


def dot_wide(a, b):
    r = dot(a, jnp.concatenate(split(b), axis=1))
    return r[:, :LANES] + r[:, LANES:]


def each(count, body):
    if count <= 8:
        for i in range(count):
            body(i)
    else:
        lax.fori_loop(0, count, lambda i, c: (body(i), c)[1], 0)


def rows_lanes(rows):
    return lax.broadcasted_iota(jnp.int32, (rows, LANES), 1)


def invert(qs, w):
    count = len(qs)
    lane = rows_lanes(w)
    row = lax.broadcasted_iota(jnp.int32, (w, LANES), 0)
    per = LANES // w
    tiles = count // per
    zero = jnp.zeros((w, LANES), f32)
    out = [[zero] * tiles for _ in range(count)]
    groups = []
    for b in range(count):
        home = jnp.where(lane == row + (b % per) * w, 1.0, 0.0)
        groups.append(([b], [qs[b]], -qs[b], {b // per: home}))
    while len(groups) > 1:
        merged = []
        last = len(groups) == 2
        for (ia, ra, da, ga), (ib, rb, db, gb) in zip(groups[::2], groups[1::2]):
            lhs = jnp.concatenate([*rb, db], axis=0).astype(bf16)[:, :w]
            tags = sorted(ga)
            rhs = jnp.concatenate([da] + [ga[t] for t in tags], axis=1).astype(bf16)
            res = dot(lhs, rhs)
            for i, b in enumerate(ib):
                for j, t in enumerate(tags):
                    part = res[w * i : w * (i + 1), LANES * (j + 1) : LANES * (j + 2)]
                    out[b][t] = out[b][t] - part
            if last:
                continue
            tail = w * len(ib)
            moved = [rb[i] + res[w * i : w * (i + 1), :LANES] for i in range(len(ib))]
            g = {t: ga[t] + res[tail:, LANES * (j + 1) : LANES * (j + 2)] for j, t in enumerate(tags)}
            for t in gb:
                g[t] = g[t] + gb[t] if t in g else gb[t]
            merged.append((ia + ib, ra + moved, da + db + res[tail:, :LANES], g))
        groups = merged
        if last:
            break
    return jnp.concatenate(
        [jnp.concatenate(parts, axis=1) for parts in out], axis=0
    ).astype(bf16)


def kernel(
    R, nb, bs, w, n,
    rhs_h, linv_h, llt_h, lrt_h, uinv_h, ult_h, urt_h, ranks_h,
    first, second,
    rhs, llt, lrt, ult, urt, ranks,
    inv, cm, wp, y, x1, x2, t1, t2, send0, send1, got0, got1, states,
    load_sem, block_sem, send_sem, recv_sem,
):
    me = lax.axis_index("rows")
    small = [
        pltpu.make_async_copy(src, dst, load_sem.at[i])
        for i, (src, dst) in enumerate(
            ((llt_h, llt), (lrt_h, lrt), (ranks_h, ranks), (rhs_h, rhs), (ult_h, ult), (urt_h, urt))
        )
    ]
    large = [
        [
            pltpu.make_async_copy(src.at[b], inv.at[f, b, 0:bs], block_sem.at[f, b])
            for b in (range(nb) if f == 0 else reversed(range(nb)))
        ]
        for f, src in ((0, linv_h), (1, uinv_h))
    ]
    for cp in small[:4] + large[0] + small[4:] + large[1]:
        cp.start()

    barrier = pltpu.get_barrier_semaphore()

    def greet(i):
        pl.semaphore_signal(
            barrier, inc=1, device_id={"rows": lax.rem(me + i + 1, R)}, device_id_type=MESH
        )

    each(R - 1, greet)

    lane = rows_lanes(w)
    row = lax.broadcasted_iota(jnp.int32, (w, LANES), 0)
    eye = jnp.where(lane == row, 1.0, 0.0)
    a_end, v_end = w, w + n
    zero = jnp.zeros((w, LANES), f32)

    def block(f, p):
        return p if f == 0 else nb - 1 - p

    def between(rows, lo, hi):
        l = rows_lanes(rows)
        return (l >= lo) & (l < hi)

    def part(x, p):
        return x[p * w : (p + 1) * w]

    lefts, rights = (llt, ult), (lrt, urt)

    def prepare(f):
        qs, us, pushed = [], [], {}
        wide_row = lax.broadcasted_iota(jnp.int32, (w, bs), 0)
        for p in range(nb):
            b = block(f, p)
            large[f][p].wait()
            base = inv[f, b, 0:bs]
            mt = jnp.where(wide_row < ranks[f, b], rights[f][b].astype(f32), 0.0).astype(bf16)
            if f == 0:
                z = dot_nt(base, jnp.concatenate([lefts[f][b], rhs[:, b * bs : (b + 1) * bs]], axis=0))
            else:
                z = dot_nt(base, lefts[f][b])
            z = jnp.concatenate([z, jnp.zeros((bs, LANES - z.shape[1]), f32)], axis=1)
            hi, lo = split(z)
            cm[f, b] = hi
            if f == 0:
                lo = jnp.where(rows_lanes(bs) < w, jnp.zeros_like(lo), lo)
                r = dot(mt, jnp.concatenate([hi, lo], axis=1))
                r = r[:, :LANES] + r[:, LANES:]
                pushed[b] = jnp.where(rows_lanes(bs) < w, 0.0, z)
            else:
                r = dot(mt, hi)
            qs.append(jnp.where(lane < w, r, 0.0))
            us.append(jnp.where(lane < w, -r, r))
            hi, lo = split(dot(mt, base))
            inv[f, b, bs : bs + w] = hi
            inv[f, b, bs + w : bs + 2 * w] = lo
        return qs, us, pushed

    def advance(f, us):
        u = jnp.concatenate(us, axis=0)
        return u + dot(wp[f], u.astype(bf16))

    def total(x, count):
        s = part(x, 0)
        for p in range(1, count):
            s = s + part(x, p)
        return s

    def coupled(f, b, s):
        return dot_wide(cm[f, b][:, :w], s)

    def push(f, src):
        us, pushed = [], {}
        for p in range(nb):
            b = block(f, p)
            r = dot_wide(inv[f, b], src[b])
            pushed[b] = r[:bs]
            us.append(r[bs : bs + w] + r[bs + w :])
        return advance(f, us), pushed

    def solve(f, wv, pushed, dst, plus=None):
        s = None
        for p in range(nb):
            b = block(f, p)
            out = pushed[b]
            if s is not None:
                out = out - coupled(f, b, s)
            if plus is not None:
                out = out + plus(b)
            dst[b] = out
            s = part(wv, p) if s is None else s + part(wv, p)

    for cp in small[:4]:
        cp.wait()
    qs, us, pushed = prepare(0)
    wp[0] = invert(qs, w)
    w_a = advance(0, us)
    end_a = total(w_a, nb)
    s = eye
    for p in range(nb):
        y[p] = pushed[p] - coupled(0, p, s)
        s = s + part(w_a, p)

    for cp in small[4:]:
        cp.wait()
    qs, us, _ = prepare(1)
    wp[1] = invert(qs, w)
    w_u = advance(1, us)
    end_u = jnp.where(lane < w, total(w_u, nb), 0.0)
    s = eye
    for p in range(nb):
        b = block(1, p)
        x1[b] = -coupled(1, b, pltpu.roll(s, v_end, 1))
        s = s + jnp.where(lane < w, part(w_u, p), 0.0)

    w_b, pushed = push(1, y)
    end_b = total(w_b, nb)
    tile0 = (
        jnp.where(lane < v_end, end_a, 0.0)
        + pltpu.roll(end_u, v_end, 1)
        + pltpu.roll(jnp.where(lane < v_end, end_b, 0.0), v_end + w, 1)
    )
    send0[...] = tile0.astype(bf16)

    def copy(k, src, dst, i):
        peer = lax.rem(me + i + 1, R)
        return pltpu.make_async_remote_copy(
            src_ref=src, dst_ref=dst.at[me], send_sem=send_sem.at[k, i],
            recv_sem=recv_sem.at[k, me], device_id={"rows": peer}, device_id_type=MESH,
        )

    def arrive(k, src, dst, i):
        peer = lax.rem(me + i + 1, R)
        pltpu.make_async_remote_copy(
            src_ref=src, dst_ref=dst.at[peer], send_sem=send_sem.at[k, i],
            recv_sem=recv_sem.at[k, peer], device_id={"rows": peer}, device_id_type=MESH,
        ).wait_recv()

    pl.semaphore_wait(barrier, R - 1)
    each(R - 1, lambda i: copy(0, send0, got0, i).start())
    got0[me] = send0[...]

    solve(1, w_b, pushed, x1, plus=lambda b: x1[b])
    w_c, pushed = push(0, x1)
    send1[:w] = total(w_c, nb).astype(bf16)
    solve(0, w_c, pushed, y)
    w_d, pushed = push(1, y)
    send1[w:] = total(w_d, nb).astype(bf16)
    each(R - 1, lambda i: copy(1, send1, got1, i).start())
    got1[me] = send1[...]

    solve(1, w_d, pushed, x2)

    def flip(src, dst):
        for b in range(nb):
            hi, lo = split(src[b].T)
            dst[b, :LANES] = hi
            dst[b, LANES:] = lo

    flip(x1, t1)
    flip(x2, t2)

    spot = jnp.where((lane == row + w) & (row < n), 1.0, 0.0)[:n]
    gap_n = jnp.zeros((n, LANES), f32)

    def stack(a, v, u, b, t):
        parts = [zero if a is None else a, gap_n if v is None else v, zero if u is None else u]
        parts += [zero if b is None else b, gap_n if t is None else t]
        return jnp.concatenate(parts, axis=0)

    def times(tile, x):
        hi, lo = split(x)
        return dot(tile, hi) + dot(tile, lo)

    each(R - 1, lambda i: arrive(0, send0, got0, i))
    if R <= 8:
        def sweep(wv, order):
            s, out = zero, [None] * R
            for i, d in enumerate(order):
                out[d] = s
                s = s + part(wv, i)
            return out

        up, down = list(range(R)), list(range(R - 1, -1, -1))
        tiles = [got0[d] for d in range(R)]
        wide = [t.astype(f32) for t in tiles]
        inner = lane < w
        fwd = invert([jnp.where(inner, -wide[d], 0.0) for d in up], w)
        bwd = invert(
            [jnp.where(inner, -pltpu.roll(wide[d], LANES - v_end, 1), 0.0) for d in down], w
        )

        def carry(m, inverse, order):
            u = jnp.concatenate([m[d] for d in order], axis=0)
            return sweep(u + dot(inverse, u.astype(bf16)), order)

        mid = between(w, w, v_end)
        s1 = carry([jnp.where(mid, wide[d], 0.0) for d in up], fwd, up)
        m2 = [dot(tiles[d], stack(None, None, None, s1[d], spot).astype(bf16)) for d in up]
        s2 = carry(m2, bwd, down)
        for d in up:
            states[0, d * w : (d + 1) * w] = s1[d]
            states[1, d * w : (d + 1) * w] = s2[d]
        each(R - 1, lambda i: arrive(1, send1, got1, i))
        m34 = [dot(got1[d], stack(s1[d], spot, s2[d], None, None).astype(bf16)) for d in up]
        s3 = carry([m34[d][:w] for d in up], fwd, up)
        m4 = [
            m34[d][w:] + dot(tiles[d], stack(None, None, None, s3[d], None).astype(bf16))
            for d in up
        ]
        s4 = carry(m4, bwd, down)
        for d in up:
            states[2, d * w : (d + 1) * w] = s3[d]
            states[3, d * w : (d + 1) * w] = s4[d]
    else:
        each(R - 1, lambda i: arrive(1, send1, got1, i))

        def at(d):
            return pl.ds(pl.multiple_of(d * w, w), w)

        def walk(k, step, back):
            def body(i, s):
                d = R - 1 - i if back else i
                states[k, at(d)] = s
                return s + step(d, s)

            lax.fori_loop(0, R, body, zero)

        def joint(d):
            return stack(states[0, at(d)], spot, states[1, at(d)], None, None)

        walk(0, lambda d, s: times(got0[d], stack(s, spot, None, None, None)), False)
        walk(1, lambda d, s: times(got0[d], stack(None, None, s, states[0, at(d)], spot)), True)
        walk(
            2,
            lambda d, s: times(got1[d, :w], joint(d))
            + times(got0[d], stack(s, None, None, None, None)),
            False,
        )
        walk(
            3,
            lambda d, s: times(got1[d, w:], joint(d))
            + times(got0[d], stack(None, None, s, states[2, at(d)], None)),
            True,
        )

    mine = pl.ds(pl.multiple_of(me * w, w), w)
    own = [states[k, mine] for k in range(4)]

    def weights(x):
        hi, lo = split(x.T[w:v_end])
        both = jnp.concatenate([hi, lo], axis=0)
        return jnp.concatenate([both, both], axis=1)

    one = weights(stack(own[0], spot, own[1], None, None))
    two = weights(stack(own[2], None, own[3], None, None))
    lhs = jnp.concatenate([one, two], axis=0)
    for b in range(nb):
        r = dot(lhs, t1[b])
        q = dot(one, t2[b])
        first[:, b * bs : (b + 1) * bs] = r[:n] + r[n : 2 * n]
        second[:, b * bs : (b + 1) * bs] = r[2 * n : 3 * n] + r[3 * n :] + q[:n] + q[n:]

    each(R - 1, lambda i: copy(0, send0, got0, i).wait_send())
    each(R - 1, lambda i: copy(1, send1, got1, i).wait_send())


def local(R, rhs, linv, lleft, lright, uinv, uleft, uright, ranks):
    nb, bs, w = lleft.shape
    n = rhs.shape[0]
    flip = lambda a: jnp.swapaxes(a, 1, 2)
    vmem = pl.BlockSpec(memory_space=pltpu.VMEM)
    hbm = pl.BlockSpec(memory_space=pltpu.HBM)
    out = jax.ShapeDtypeStruct(rhs.shape, f32)
    slim = pltpu.VMEM((nb, w, bs), bf16)
    tall = pltpu.VMEM((nb, bs, LANES), f32)
    args = (rhs, linv, flip(lleft), flip(lright), uinv, flip(uleft), flip(uright), ranks)
    return pl.pallas_call(
        functools.partial(kernel, R, nb, bs, w, n),
        out_shape=(out, out),
        in_specs=[hbm] * 8,
        out_specs=(vmem, vmem),
        scratch_shapes=[
            pltpu.VMEM(rhs.shape, bf16),
            slim, slim, slim, slim,
            pltpu.SMEM(ranks.shape, jnp.int32),
            pltpu.VMEM((2, nb, bs + 2 * w, bs), bf16),
            pltpu.VMEM((2, nb, bs, LANES), bf16),
            pltpu.VMEM((2, nb * w, nb * w), bf16),
            tall, tall, tall,
            pltpu.VMEM((nb, 2 * LANES, bs), bf16),
            pltpu.VMEM((nb, 2 * LANES, bs), bf16),
            pltpu.VMEM((w, LANES), bf16),
            pltpu.VMEM((2 * w, LANES), bf16),
            pltpu.VMEM((R, w, LANES), bf16),
            pltpu.VMEM((R, 2 * w, LANES), bf16),
            pltpu.VMEM((4, R * w, LANES), f32),
            pltpu.SemaphoreType.DMA((6,)),
            pltpu.SemaphoreType.DMA((2, nb)),
            pltpu.SemaphoreType.DMA((2, R)),
            pltpu.SemaphoreType.DMA((2, R)),
        ],
        compiler_params=pltpu.CompilerParams(
            collective_id=0, has_side_effects=True, vmem_limit_bytes=33554432
        ),
    )(*[pltpu.with_memory_space_constraint(a, pltpu.HBM) for a in args])


def solution(mesh):
    blocks = P("rows", None, None)
    placed = (P("rhs", "rows"),) + (blocks,) * 6 + (P(None, "rows"),)
    return jax.shard_map(
        functools.partial(local, mesh.shape["rows"]),
        mesh=mesh,
        in_specs=placed,
        out_specs=(P("rhs", "rows"), P("rhs", "rows")),
        check_vma=False,
    )
```

time: 27.2 us -> 23.1 us (0.85)
  Pallas kernels: 25.1 us -> 21 us
    pallas_call x1, Pallas kernels: 25.1 us -> 21 us  [local(): pl.pallas_call(functools.partial(kernel, R, nb, bs, w, n), out_shape=(out...]
where the time goes in v3:
time: 23.1 us; the launch traced here: 23 us
  Pallas kernels  21 us (91%)
  local copies, waits for them, and re-layouts  1.31 us (6%)
  between operations  0.64 us (3%)
    pallas_call x1, Pallas kernels, local(): pl.pallas_call(functools.partial(kernel, R, nb, bs, w, n), out_shape=(out...  21 us
    unnamed x2, local copies, waits for them, and re-layouts  1.31 us

profile of v3, /device:TPU:0, one launch (start us, length us, event | category | flops | bytes accessed | tf_op | source)
XLA Modules:
  0.0 23.0 jit_solution(6527147733091935741)
XLA Ops:
  0.6 21.0 %shard_map.95 = (f32[16,2048]{1,0:T(8,128)S(1)}, f32[16,2048]{1,0:T(8,128)S(1)}) custom-call(bf16[16,2048]{1,0:T(8,128)(2,1)} %rhs_h.1, bf16[8,256,256]{2,1,0:T(8,128)(2,1)} %linv_h.1, bf16[8,32,256]{2,1,0:T(8,128)(2,1)} %bitcast.4, bf16[8,32,256]{2,1,0:T(8,128)(2,1)} %bitcast.5, bf16[8,256,256]{2,1,0:T(8,128)(2,1)} %uinv_h.1, bf16[8,32,256]{2,1,0:T(8,128)(2,1)} %bitcast.6, ...), custom_call_target="tpu_custom_call" | custom-call | tf_op jit(solution)/shard_map/pallas_call | solution.py:385
  21.7 0.7 %copy.12 = f32[16,2048]{1,0:T(8,128)} copy(f32[16,2048]{1,0:T(8,128)S(1)} %get-tuple-element.4) | data formatting | bytes 262144
  22.3 0.7 %copy.13 = f32[16,2048]{1,0:T(8,128)} copy(f32[16,2048]{1,0:T(8,128)S(1)} %get-tuple-element.5) | data formatting | bytes 262144

commit v4 on v3

v4 whole, which is shorter than its diff:
```python
import functools

import jax
import jax.numpy as jnp
from jax import lax
from jax.experimental import pallas as pl
from jax.experimental.pallas import tpu as pltpu
from jax.sharding import PartitionSpec as P

MESH = pl.DeviceIdType.MESH
LANES = 128
f32, bf16 = jnp.float32, jnp.bfloat16


def split(x):
    hi = x.astype(bf16)
    return hi, (x - hi.astype(f32)).astype(bf16)


def dot(a, b):
    return jnp.dot(a, b, preferred_element_type=f32)


def dot_nt(a, b):
    return lax.dot_general(a, b, (((1,), (1,)), ((), ())), preferred_element_type=f32)


def each(count, body):
    if count <= 8:
        for i in range(count):
            body(i)
    else:
        lax.fori_loop(0, count, lambda i, c: (body(i), c)[1], 0)


def rows_lanes(rows):
    return lax.broadcasted_iota(jnp.int32, (rows, LANES), 1)


def invert_steps(qs, w, out):
    count = len(qs)
    lane = rows_lanes(w)
    row = lax.broadcasted_iota(jnp.int32, (w, LANES), 0)
    per = LANES // w
    tiles = count // per
    zero = jnp.zeros((w, LANES), f32)
    out.extend([zero] * tiles for _ in range(count))
    groups = []
    for b in range(count):
        home = jnp.where(lane == row + (b % per) * w, 1.0, 0.0)
        groups.append(([b], [qs[b]], -qs[b], {b // per: home}))
    while len(groups) > 1:
        merged = []
        last = len(groups) == 2
        for (ia, ra, da, ga), (ib, rb, db, gb) in zip(groups[::2], groups[1::2]):
            lhs = jnp.concatenate(rb if last else [*rb, db], axis=0).astype(bf16)[:, :w]
            tags = sorted(ga)
            rhs = jnp.concatenate([ga[t] for t in tags] + ([] if last else [da]), axis=1).astype(bf16)
            res = dot(lhs, rhs)
            at = len(tags) * LANES
            for i, b in enumerate(ib):
                for j, t in enumerate(tags):
                    out[b][t] = out[b][t] - res[w * i : w * (i + 1), LANES * j : LANES * (j + 1)]
            if last:
                continue
            tail = w * len(ib)
            moved = [rb[i] + res[w * i : w * (i + 1), at:] for i in range(len(ib))]
            g = {t: ga[t] + res[tail:, LANES * j : LANES * (j + 1)] for j, t in enumerate(tags)}
            for t in gb:
                g[t] = g[t] + gb[t] if t in g else gb[t]
            merged.append((ia + ib, ra + moved, da + db + res[tail:, at:], g))
        groups = merged
        yield
        if last:
            break


def together(*steps):
    live = list(steps)
    while live:
        live = [s for s in live if next(s, s) is not s]


def joined(out):
    return jnp.concatenate([jnp.concatenate(parts, axis=1) for parts in out], axis=0)


def kernel(
    R, nb, bs, w, n,
    rhs_h, linv_h, llt_h, lrt_h, uinv_h, ult_h, urt_h, ranks_h,
    first, second,
    rhs, llt, lrt, ult, urt, ranks,
    inv, cm, wp, y, x1, x2, t1, t2, send0, send1, got0, got1, states,
    load_sem, block_sem, send_sem, recv_sem,
):
    me = lax.axis_index("rows")
    small = [
        pltpu.make_async_copy(src, dst, load_sem.at[i])
        for i, (src, dst) in enumerate(
            ((lrt_h, lrt), (ranks_h, ranks), (llt_h, llt), (rhs_h, rhs), (urt_h, urt), (ult_h, ult))
        )
    ]
    large = [
        [
            pltpu.make_async_copy(src.at[b], inv.at[f, b, 0:bs], block_sem.at[f, b])
            for b in range(nb)
        ]
        for f, src in ((0, linv_h), (1, uinv_h))
    ]
    for cp in small[:4] + large[0] + small[4:] + large[1]:
        cp.start()

    barrier = pltpu.get_barrier_semaphore()

    def greet(i):
        pl.semaphore_signal(
            barrier, inc=1, device_id={"rows": lax.rem(me + i + 1, R)}, device_id_type=MESH
        )

    each(R - 1, greet)

    lane = rows_lanes(w)
    row = lax.broadcasted_iota(jnp.int32, (w, LANES), 0)
    v_at, lo_at, v_end = 2 * w, 2 * w + n, 2 * w + 2 * n
    zero = jnp.zeros((w, LANES), f32)
    gap = jnp.zeros((n, LANES), f32)
    eye_l = jnp.where(lane == row, 1.0, 0.0)
    eye_u = jnp.where(lane == row + w, 1.0, 0.0)
    n_hi, n_lo, adj = bs, bs + w, bs + 2 * w

    def block(f, p):
        return p if f == 0 else nb - 1 - p

    def between(rows, lo, hi):
        l = rows_lanes(rows)
        return (l >= lo) & (l < hi)

    def part(x, p):
        return x[p * w : (p + 1) * w]

    lefts, rights = (llt, ult), (lrt, urt)

    def reduce_left(f):
        wide_row = lax.broadcasted_iota(jnp.int32, (w, bs), 0)
        tall = []
        for p in range(nb):
            b = block(f, p)
            mt = jnp.where(wide_row < ranks[f, b], rights[f][b].astype(f32), 0.0).astype(bf16)
            t = dot(mt, inv[f, b, 0:bs])
            hi, lo = split(t)
            inv[f, b, n_hi:n_lo] = hi
            inv[f, b, n_lo:adj] = lo
            tall.append(t)
        return tall

    def prepare(f):
        qs, us, pushed = [], [], {}
        for p in range(nb):
            b = block(f, p)
            left = lefts[f][b]
            if f == 0:
                v = rhs[:, b * bs : (b + 1) * bs]
                cols = jnp.concatenate([left, left, v, v], axis=0)
            else:
                cols = jnp.concatenate([left, left], axis=0)
            z = dot_nt(inv[f, b, 0:adj], cols)
            z = jnp.concatenate([z, jnp.zeros((adj, LANES - z.shape[1]), f32)], axis=1)
            cm[f, b] = z[:bs].astype(bf16)
            pushed[b] = z[:bs]
            r = z[n_hi:n_lo] + z[n_lo:]
            qs.append(jnp.where(lane < w, r, 0.0))
            if f == 0:
                us.append(jnp.where(lane < w, -r, jnp.where(lane < v_at, 0.0, r)))
            else:
                us.append(jnp.where((lane >= w) & (lane < v_at), -r, 0.0))
        return qs, us, pushed

    def advance(f, us):
        u = jnp.concatenate(us, axis=0)
        return u + dot(wp[f], u.astype(bf16))

    def total(x, count):
        s = part(x, 0)
        for p in range(1, count):
            s = s + part(x, p)
        return s

    def coupled(f, b, s):
        return dot(cm[f, b][:, : 2 * w], jnp.concatenate(split(s), axis=0))

    def push(f, src, count):
        us, pushed = [], {}
        for p in range(nb):
            b = block(f, p)
            r = dot(inv[f, b, 0:adj], src(b))
            pushed[b] = r[:bs]
            us.append(r[n_hi:n_lo] + r[n_lo:])
        return us, pushed

    def solve(f, wv, pushed, dst, s=None):
        for p in range(nb):
            b = block(f, p)
            dst[b] = pushed[b] if s is None else pushed[b] - coupled(f, b, s)
            s = part(wv, p) if s is None else s + part(wv, p)

    def columns(x):
        hi = x.astype(bf16)
        l = rows_lanes(bs)
        rest = x - hi.astype(f32)
        low = jnp.where(between(bs, lo_at, v_end), x + pltpu.roll(rest, n, 1), x)
        return low.astype(bf16)

    for cp in small[:2]:
        cp.wait()
    for cp in small[2:4]:
        cp.wait()
    for cp in large[0]:
        cp.wait()
    reduce_left(0)
    for cp in small[4:]:
        cp.wait()
    for cp in large[1]:
        cp.wait()
    tall_u = reduce_left(1)
    qs_l, us_l, z_l = prepare(0)
    qs_u, us_u, _ = prepare(1)
    out_l, out_u = [], []
    together(invert_steps(qs_l, w, out_l), invert_steps(qs_u, w, out_u))
    wp[0] = joined(out_l).astype(bf16)
    dev_u = joined(out_u)
    wp[1] = dev_u.astype(bf16)
    w_a = advance(0, us_l)
    w_u = advance(1, us_u)

    top = total(dev_u, nb)
    spread = jnp.concatenate([top] * nb, axis=0)
    r_id = lax.broadcasted_iota(jnp.int32, spread.shape, 0) // w
    c_id = lax.broadcasted_iota(jnp.int32, spread.shape, 1) // w
    stacked = jnp.concatenate(tall_u, axis=0)
    adjoint = stacked + dot(
        jnp.where(r_id == c_id, spread, 0.0).astype(bf16), stacked.astype(bf16)
    )
    turn = {}

    s = eye_l
    for p in range(nb):
        y[p] = jnp.where(between(bs, v_at, v_end), z_l[p], 0.0) - coupled(0, p, s)
        s = s + part(w_a, p)
        b = p
        a = part(adjoint, block(1, b)).astype(bf16)
        inv[0, b, adj:] = dot(a, inv[0, b, 0:bs]).astype(bf16)
        turn[b] = dot(a, cm[0, b]).astype(bf16)[:, :w]

    def twin(b):
        x = y[b]
        hi = x.astype(bf16)
        return jnp.where(between(bs, lo_at, v_end), x - hi.astype(f32), x).astype(bf16)

    us, pushed = push(1, twin, nb)
    w_b = advance(1, us)
    end_a, end_u, end_b = total(w_a, nb), total(w_u, nb), total(w_b, nb)
    shift = pltpu.roll(end_b, n, 1)
    tile0 = jnp.where(lane < w, end_a, end_u)
    tile0 = jnp.where(between(w, v_at, lo_at), end_a, tile0)
    tile0 = jnp.where(between(w, lo_at, v_end), end_b + shift, tile0)
    tile0 = jnp.where(lane >= v_end, pltpu.roll(end_b, v_end, 1), tile0)
    send0[...] = tile0.astype(bf16)

    def copy(k, src, dst, i):
        peer = lax.rem(me + i + 1, R)
        return pltpu.make_async_remote_copy(
            src_ref=src, dst_ref=dst.at[me], send_sem=send_sem.at[k, i],
            recv_sem=recv_sem.at[k, me], device_id={"rows": peer}, device_id_type=MESH,
        )

    def arrive(k, src, dst, i):
        peer = lax.rem(me + i + 1, R)
        pltpu.make_async_remote_copy(
            src_ref=src, dst_ref=dst.at[peer], send_sem=send_sem.at[k, i],
            recv_sem=recv_sem.at[k, peer], device_id={"rows": peer}, device_id_type=MESH,
        ).wait_recv()

    pl.semaphore_wait(barrier, R - 1)
    each(R - 1, lambda i: copy(0, send0, got0, i).start())
    got0[me] = send0[...]

    solve(1, w_b + w_u, pushed, x1, eye_u)
    us, direct = [], None
    for b in range(nb):
        r = dot(inv[0, b, n_hi:], x1[b].astype(bf16))
        us.append(r[:w] + r[w : 2 * w])
        direct = r[2 * w :] if direct is None else direct + r[2 * w :]
    w_c = advance(0, us)
    send1[:w] = total(w_c, nb).astype(bf16)
    s = part(w_c, 0)
    crossed = None
    for b in range(1, nb):
        t = dot(turn[b], s.astype(bf16))
        crossed = t if crossed is None else crossed + t
        s = s + part(w_c, b)
    send1[w:] = (direct - crossed).astype(bf16)
    each(R - 1, lambda i: copy(1, send1, got1, i).start())
    got1[me] = send1[...]

    us, pushed = push(0, lambda b: columns(x1[b]), nb)
    solve(0, advance(0, us), pushed, y)
    us, pushed = push(1, lambda b: columns(y[b]), nb)
    solve(1, advance(1, us), pushed, x2)

    def flip(src, dst):
        for b in range(nb):
            hi, lo = split(src[b].T)
            dst[b, :LANES] = hi
            dst[b, LANES:] = lo

    flip(x1, t1)
    flip(x2, t2)

    spot = jnp.where((lane == row + v_at) & (row < n), 1.0, 0.0)[:n]

    def near(a, b, own):
        a, b = (zero if a is None else a), (zero if b is None else b)
        v = spot if own else gap
        return jnp.concatenate([a, b, v, v, zero], axis=0)

    def late(b, own, a=None):
        return jnp.concatenate(
            [zero, zero if a is None else a, gap, spot if own else gap, b], axis=0
        )

    def times(tile, x):
        hi, lo = split(x)
        return dot(tile, hi) + dot(tile, lo)

    def weights(x):
        hi, lo = split(x.T[v_at:lo_at])
        both = jnp.concatenate([hi, lo], axis=0)
        return jnp.concatenate([both, both], axis=1)

    def halves(r):
        return r[:n] + r[n:]

    mine = pl.ds(pl.multiple_of(me * w, w), w)

    def opening():
        one = weights(near(states[0, mine], states[1, mine], True))
        for b in range(nb):
            at = slice(b * bs, (b + 1) * bs)
            first[:, at] = halves(dot(one, t1[b]))
            second[:, at] = halves(dot(one, t2[b]))

    each(R - 1, lambda i: arrive(0, send0, got0, i))
    if R <= 8:
        def sweep(wv, order):
            s, out = zero, [None] * R
            for i, d in enumerate(order):
                out[d] = s
                s = s + part(wv, i)
            return out

        up, down = list(range(R)), list(range(R - 1, -1, -1))
        tiles = [got0[d] for d in range(R)]
        wide = [t.astype(f32) for t in tiles]
        inner = lane < w
        out_f, out_b = [], []
        together(
            invert_steps([jnp.where(inner, -wide[d], 0.0) for d in up], w, out_f),
            invert_steps(
                [jnp.where(inner, -pltpu.roll(wide[d], LANES - w, 1), 0.0) for d in down], w, out_b
            ),
        )
        fwd, bwd = joined(out_f).astype(bf16), joined(out_b).astype(bf16)

        def carry(m, inverse, order):
            u = jnp.concatenate([m[d] for d in order], axis=0)
            return sweep(u + dot(inverse, u.astype(bf16)), order)

        mid = between(w, v_at, lo_at)
        s1 = carry([jnp.where(mid, wide[d], 0.0) for d in up], fwd, up)
        m2 = [dot(tiles[d], late(s1[d], True).astype(bf16)) for d in up]
        s2 = carry(m2, bwd, down)
        for d in up:
            states[0, d * w : (d + 1) * w] = s1[d]
            states[1, d * w : (d + 1) * w] = s2[d]
        opening()
        each(R - 1, lambda i: arrive(1, send1, got1, i))
        m34 = [dot(got1[d], near(s1[d], s2[d], True).astype(bf16)) for d in up]
        s3 = carry([m34[d][:w] for d in up], fwd, up)
        m4 = [m34[d][w:] + dot(tiles[d], late(s3[d], False).astype(bf16)) for d in up]
        s4 = carry(m4, bwd, down)
        for d in up:
            states[2, d * w : (d + 1) * w] = s3[d]
            states[3, d * w : (d + 1) * w] = s4[d]
    else:
        def at(d):
            return pl.ds(pl.multiple_of(d * w, w), w)

        def walk(k, step, back):
            def body(i, s):
                d = R - 1 - i if back else i
                states[k, at(d)] = s
                return s + step(d, s)

            lax.fori_loop(0, R, body, zero)

        def joint(d):
            return near(states[0, at(d)], states[1, at(d)], True)

        def ahead(s, own):
            v = spot if own else gap
            return jnp.concatenate([s, zero, v, gap, zero], axis=0)

        walk(0, lambda d, s: times(got0[d], ahead(s, True)), False)
        walk(1, lambda d, s: times(got0[d], late(states[0, at(d)], True, s)), True)
        opening()
        each(R - 1, lambda i: arrive(1, send1, got1, i))
        walk(
            2,
            lambda d, s: times(got1[d, :w], joint(d)) + times(got0[d], ahead(s, False)),
            False,
        )
        walk(
            3,
            lambda d, s: times(got1[d, w:], joint(d))
            + times(got0[d], late(states[2, at(d)], False, s)),
            True,
        )

    two = weights(near(states[2, mine], states[3, mine], False))
    for b in range(nb):
        at = slice(b * bs, (b + 1) * bs)
        second[:, at] = second[:, at] + halves(dot(two, t1[b]))

    each(R - 1, lambda i: copy(0, send0, got0, i).wait_send())
    each(R - 1, lambda i: copy(1, send1, got1, i).wait_send())


def local(R, rhs, linv, lleft, lright, uinv, uleft, uright, ranks):
    nb, bs, w = lleft.shape
    n = rhs.shape[0]
    flip = lambda a: jnp.swapaxes(a, 1, 2)
    vmem = pl.BlockSpec(memory_space=pltpu.VMEM)
    hbm = pl.BlockSpec(memory_space=pltpu.HBM)
    out = jax.ShapeDtypeStruct(rhs.shape, f32)
    slim = pltpu.VMEM((nb, w, bs), bf16)
    tall = pltpu.VMEM((nb, bs, LANES), f32)
    args = (rhs, linv, flip(lleft), flip(lright), uinv, flip(uleft), flip(uright), ranks)
    return pl.pallas_call(
        functools.partial(kernel, R, nb, bs, w, n),
        out_shape=(out, out),
        in_specs=[hbm] * 8,
        out_specs=(vmem, vmem),
        scratch_shapes=[
            pltpu.VMEM(rhs.shape, bf16),
            slim, slim, slim, slim,
            pltpu.SMEM(ranks.shape, jnp.int32),
            pltpu.VMEM((2, nb, bs + 3 * w, bs), bf16),
            pltpu.VMEM((2, nb, bs, LANES), bf16),
            pltpu.VMEM((2, nb * w, nb * w), bf16),
            tall, tall, tall,
            pltpu.VMEM((nb, 2 * LANES, bs), bf16),
            pltpu.VMEM((nb, 2 * LANES, bs), bf16),
            pltpu.VMEM((w, LANES), bf16),
            pltpu.VMEM((2 * w, LANES), bf16),
            pltpu.VMEM((R, w, LANES), bf16),
            pltpu.VMEM((R, 2 * w, LANES), bf16),
            pltpu.VMEM((4, R * w, LANES), f32),
            pltpu.SemaphoreType.DMA((6,)),
            pltpu.SemaphoreType.DMA((2, nb)),
            pltpu.SemaphoreType.DMA((2, R)),
            pltpu.SemaphoreType.DMA((2, R)),
        ],
        compiler_params=pltpu.CompilerParams(
            collective_id=0, has_side_effects=True, vmem_limit_bytes=33554432
        ),
    )(*[pltpu.with_memory_space_constraint(a, pltpu.HBM) for a in args])


def solution(mesh):
    blocks = P("rows", None, None)
    placed = (P("rhs", "rows"),) + (blocks,) * 6 + (P(None, "rows"),)
    return jax.shard_map(
        functools.partial(local, mesh.shape["rows"]),
        mesh=mesh,
        in_specs=placed,
        out_specs=(P("rhs", "rows"), P("rhs", "rows")),
        check_vma=False,
    )
```

time: 23.1 us -> 17.7 us (0.77)
  Pallas kernels: 21 us -> 15.6 us
    pallas_call x1, Pallas kernels: 21 us -> 15.6 us  [local(): pl.pallas_call(functools.partial(kernel, R, nb, bs, w, n), out_shape=(out...]
where the time goes in v4:
time: 17.7 us; the launch traced here: 17.6 us
  Pallas kernels  15.6 us (88%)
  local copies, waits for them, and re-layouts  1.31 us (7%)
  between operations  0.64 us (4%)
    pallas_call x1, Pallas kernels, local(): pl.pallas_call(functools.partial(kernel, R, nb, bs, w, n), out_shape=(out...  15.6 us
    unnamed x2, local copies, waits for them, and re-layouts  1.31 us

profile of v4, /device:TPU:0, one launch (start us, length us, event | category | flops | bytes accessed | tf_op | source)
XLA Modules:
  0.0 17.6 jit_solution(905264263088658447)
XLA Ops:
  0.6 15.6 %shard_map.95 = (f32[16,2048]{1,0:T(8,128)S(1)}, f32[16,2048]{1,0:T(8,128)S(1)}) custom-call(bf16[16,2048]{1,0:T(8,128)(2,1)} %rhs_h.1, bf16[8,256,256]{2,1,0:T(8,128)(2,1)} %linv_h.1, bf16[8,32,256]{2,1,0:T(8,128)(2,1)} %bitcast.4, bf16[8,32,256]{2,1,0:T(8,128)(2,1)} %bitcast.5, bf16[8,256,256]{2,1,0:T(8,128)(2,1)} %uinv_h.1, bf16[8,32,256]{2,1,0:T(8,128)(2,1)} %bitcast.6, ...), custom_call_target="tpu_custom_call" | custom-call | tf_op jit(solution)/shard_map/pallas_call | solution.py:448
  16.3 0.7 %copy.12 = f32[16,2048]{1,0:T(8,128)} copy(f32[16,2048]{1,0:T(8,128)S(1)} %get-tuple-element.4) | data formatting | bytes 262144
  16.9 0.7 %copy.13 = f32[16,2048]{1,0:T(8,128)} copy(f32[16,2048]{1,0:T(8,128)S(1)} %get-tuple-element.5) | data formatting | bytes 262144

commit v5 on v4

--- a/solution.py
+++ b/solution.py
@@ -90,7 +90,7 @@
     rhs_h, linv_h, llt_h, lrt_h, uinv_h, ult_h, urt_h, ranks_h,
     first, second,
     rhs, llt, lrt, ult, urt, ranks,
-    inv, cm, wp, y, x1, x2, t1, t2, send0, send1, got0, got1, states,
+    inv, adj, cm, wp, y, x1, x2, t1, t2, send0, send1, got0, got1, states, maps,
     load_sem, block_sem, send_sem, recv_sem,
 ):
     me = lax.axis_index("rows")
@@ -126,7 +126,7 @@
     gap = jnp.zeros((n, LANES), f32)
     eye_l = jnp.where(lane == row, 1.0, 0.0)
     eye_u = jnp.where(lane == row + w, 1.0, 0.0)
-    n_hi, n_lo, adj = bs, bs + w, bs + 2 * w
+    low, full_rows = bs, bs + w
 
     def block(f, p):
         return p if f == 0 else nb - 1 - p
@@ -147,33 +147,65 @@
             b = block(f, p)
             mt = jnp.where(wide_row < ranks[f, b], rights[f][b].astype(f32), 0.0).astype(bf16)
             t = dot(mt, inv[f, b, 0:bs])
-            hi, lo = split(t)
-            inv[f, b, n_hi:n_lo] = hi
-            inv[f, b, n_lo:adj] = lo
+            inv[f, b, low:full_rows] = t.astype(bf16)
             tall.append(t)
         return tall
 
-    def prepare(f):
-        qs, us, pushed = [], [], {}
+    def lead(f):
+        qs, us = [], []
+        for p in range(nb):
+            b = block(f, p)
+            cols = lefts[f][b]
+            if f == 0:
+                cols = jnp.concatenate([cols, rhs[:, b * bs : (b + 1) * bs]], axis=0)
+            r = dot_nt(inv[f, b, low:full_rows], cols)
+            r = jnp.concatenate([r, jnp.zeros((w, LANES - r.shape[1]), f32)], axis=1)
+            qs.append(jnp.where(lane < w, r, 0.0))
+            if f == 0:
+                u = jnp.where(lane < w, -r, 0.0)
+                u = jnp.where(between(w, v_at, lo_at), pltpu.roll(r, v_at - w, 1), u)
+                us.append(jnp.where(between(w, lo_at, v_end), pltpu.roll(r, lo_at - w, 1), u))
+            else:
+                us.append(jnp.where(between(w, w, v_at), pltpu.roll(-r, w, 1), 0.0))
+        return qs, us
+
+    def couple(f, pushed, chunk):
         for p in range(nb):
             b = block(f, p)
             left = lefts[f][b]
+            cols = [left, left]
             if f == 0:
                 v = rhs[:, b * bs : (b + 1) * bs]
-                cols = jnp.concatenate([left, left, v, v], axis=0)
-            else:
-                cols = jnp.concatenate([left, left], axis=0)
-            z = dot_nt(inv[f, b, 0:adj], cols)
-            z = jnp.concatenate([z, jnp.zeros((adj, LANES - z.shape[1]), f32)], axis=1)
-            cm[f, b] = z[:bs].astype(bf16)
-            pushed[b] = z[:bs]
-            r = z[n_hi:n_lo] + z[n_lo:]
-            qs.append(jnp.where(lane < w, r, 0.0))
-            if f == 0:
-                us.append(jnp.where(lane < w, -r, jnp.where(lane < v_at, 0.0, r)))
-            else:
-                us.append(jnp.where((lane >= w) & (lane < v_at), -r, 0.0))
-        return qs, us, pushed
+                cols += [v, v]
+            z = dot_nt(inv[f, b, 0:bs], jnp.concatenate(cols, axis=0))
+            z = jnp.concatenate([z, jnp.zeros((bs, LANES - z.shape[1]), f32)], axis=1)
+            cm[f, b] = z.astype(bf16)
+            pushed[b] = z
+            if p % chunk == chunk - 1:
+                yield
+
+    per = LANES // w
+
+    def diagonal(tiles):
+        return jnp.concatenate(
+            [
+                jnp.concatenate(
+                    [
+                        jnp.where(lane // w == p % per, tiles[t], 0.0) if t == p // per else zero
+                        for t in range(len(tiles))
+                    ],
+                    axis=1,
+                )
+                for p in range(len(tiles) * per)
+            ],
+            axis=0,
+        ).astype(bf16)
+
+    def tops(out):
+        return [sum(out[p][t] for p in range(1, len(out))) for t in range(len(out[0]))]
+
+    def home(p, t):
+        return jnp.where(lane == row + p % per * w, 1.0, 0.0) if t == p // per else zero
 
     def advance(f, us):
         u = jnp.concatenate(us, axis=0)
@@ -192,9 +224,9 @@
         us, pushed = [], {}
         for p in range(nb):
             b = block(f, p)
-            r = dot(inv[f, b, 0:adj], src(b))
+            r = dot(inv[f, b, 0:full_rows], src(b))
             pushed[b] = r[:bs]
-            us.append(r[n_hi:n_lo] + r[n_lo:])
+            us.append(r[low:])
         return us, pushed
 
     def solve(f, wv, pushed, dst, s=None):
@@ -210,46 +242,53 @@
         low = jnp.where(between(bs, lo_at, v_end), x + pltpu.roll(rest, n, 1), x)
         return low.astype(bf16)
 
-    for cp in small[:2]:
+    for cp in small[:4] + large[0]:
         cp.wait()
-    for cp in small[2:4]:
-        cp.wait()
-    for cp in large[0]:
-        cp.wait()
-    reduce_left(0)
-    for cp in small[4:]:
-        cp.wait()
-    for cp in large[1]:
+    tall_l = reduce_left(0)
+    qs_l, us_l = lead(0)
+    z_l = {}
+    for _ in couple(0, z_l, nb):
+        pass
+    for cp in small[4:] + large[1]:
         cp.wait()
     tall_u = reduce_left(1)
-    qs_l, us_l, z_l = prepare(0)
-    qs_u, us_u, _ = prepare(1)
+    qs_u, us_u = lead(1)
     out_l, out_u = [], []
-    together(invert_steps(qs_l, w, out_l), invert_steps(qs_u, w, out_u))
+    together(
+        invert_steps(qs_l, w, out_l), invert_steps(qs_u, w, out_u), couple(1, {}, -(-nb // 3))
+    )
     wp[0] = joined(out_l).astype(bf16)
-    dev_u = joined(out_u)
-    wp[1] = dev_u.astype(bf16)
+    wp[1] = joined(out_u).astype(bf16)
     w_a = advance(0, us_l)
     w_u = advance(1, us_u)
-
-    top = total(dev_u, nb)
-    spread = jnp.concatenate([top] * nb, axis=0)
-    r_id = lax.broadcasted_iota(jnp.int32, spread.shape, 0) // w
-    c_id = lax.broadcasted_iota(jnp.int32, spread.shape, 1) // w
-    stacked = jnp.concatenate(tall_u, axis=0)
-    adjoint = stacked + dot(
-        jnp.where(r_id == c_id, spread, 0.0).astype(bf16), stacked.astype(bf16)
-    )
+    base_u = jnp.concatenate(tall_u, axis=0)
+    base_l = jnp.concatenate(tall_l, axis=0)
+    adjoint = base_u + dot(diagonal(tops(out_u)), base_u.astype(bf16))
+
+    s = eye_l
     turn = {}
-
-    s = eye_l
     for p in range(nb):
         y[p] = jnp.where(between(bs, v_at, v_end), z_l[p], 0.0) - coupled(0, p, s)
         s = s + part(w_a, p)
-        b = p
-        a = part(adjoint, block(1, b)).astype(bf16)
-        inv[0, b, adj:] = dot(a, inv[0, b, 0:bs]).astype(bf16)
-        turn[b] = dot(a, cm[0, b]).astype(bf16)[:, :w]
+
+    rows_a = [part(adjoint, block(1, b)).astype(bf16) for b in range(nb)]
+    for b in range(nb):
+        turn[b] = dot(rows_a[b], cm[0, b])
+    later = {nb - 1: None}
+    for b in range(nb - 1, 0, -1):
+        later[b - 1] = turn[b] if later[b] is None else later[b] + turn[b]
+    wide_y = None
+    for b in range(nb - 1):
+        full = jnp.concatenate([out_l[b][t] + home(b, t) for t in range(nb // per)], axis=1)
+        t = dot(later[b].astype(bf16)[:, :w], full.astype(bf16))
+        wide_y = t if wide_y is None else wide_y + t
+    y_tiles = [wide_y[:, t * LANES : (t + 1) * LANES] for t in range(nb // per)]
+    base_hi = base_l.astype(bf16)
+    near_rows = base_l + dot(diagonal(tops(out_l)), base_hi)
+    far_rows = dot(diagonal(y_tiles), base_hi)
+    for b in range(nb):
+        adj[b, :w] = part(near_rows, b).astype(bf16)
+        adj[b, w:] = (dot(rows_a[b], inv[0, b, 0:bs]) - part(far_rows, b)).astype(bf16)
 
     def twin(b):
         x = y[b]
@@ -266,15 +305,17 @@
     tile0 = jnp.where(lane >= v_end, pltpu.roll(end_b, v_end, 1), tile0)
     send0[...] = tile0.astype(bf16)
 
+    def peer_of(i):
+        return i + (i + R - me) // R
+
     def copy(k, src, dst, i):
-        peer = lax.rem(me + i + 1, R)
         return pltpu.make_async_remote_copy(
             src_ref=src, dst_ref=dst.at[me], send_sem=send_sem.at[k, i],
-            recv_sem=recv_sem.at[k, me], device_id={"rows": peer}, device_id_type=MESH,
+            recv_sem=recv_sem.at[k, me], device_id={"rows": peer_of(i)}, device_id_type=MESH,
         )
 
     def arrive(k, src, dst, i):
-        peer = lax.rem(me + i + 1, R)
+        peer = peer_of(i)
         pltpu.make_async_remote_copy(
             src_ref=src, dst_ref=dst.at[peer], send_sem=send_sem.at[k, i],
             recv_sem=recv_sem.at[k, peer], device_id={"rows": peer}, device_id_type=MESH,
@@ -285,36 +326,32 @@
     got0[me] = send0[...]
 
     solve(1, w_b + w_u, pushed, x1, eye_u)
-    us, direct = [], None
+    ends = None
     for b in range(nb):
-        r = dot(inv[0, b, n_hi:], x1[b].astype(bf16))
-        us.append(r[:w] + r[w : 2 * w])
-        direct = r[2 * w :] if direct is None else direct + r[2 * w :]
-    w_c = advance(0, us)
-    send1[:w] = total(w_c, nb).astype(bf16)
-    s = part(w_c, 0)
-    crossed = None
-    for b in range(1, nb):
-        t = dot(turn[b], s.astype(bf16))
-        crossed = t if crossed is None else crossed + t
-        s = s + part(w_c, b)
-    send1[w:] = (direct - crossed).astype(bf16)
+        r = dot(adj[b], x1[b].astype(bf16))
+        ends = r if ends is None else ends + r
+    send1[...] = ends.astype(bf16)
     each(R - 1, lambda i: copy(1, send1, got1, i).start())
     got1[me] = send1[...]
 
-    us, pushed = push(0, lambda b: columns(x1[b]), nb)
-    solve(0, advance(0, us), pushed, y)
-    us, pushed = push(1, lambda b: columns(y[b]), nb)
-    solve(1, advance(1, us), pushed, x2)
-
-    def flip(src, dst):
+    @pl.when(me >= 0)
+    def _():
+        def flip(dst):
+            def src(b, x):
+                cols = columns(x)
+                dst[b] = cols.T
+                return cols
+
+            return src
+
+        keep = flip(t1)
+        us, pushed = push(0, lambda b: keep(b, x1[b]), nb)
+        solve(0, advance(0, us), pushed, y)
+        us, pushed = push(1, lambda b: columns(y[b]), nb)
+        solve(1, advance(1, us), pushed, x2)
+        keep = flip(t2)
         for b in range(nb):
-            hi, lo = split(src[b].T)
-            dst[b, :LANES] = hi
-            dst[b, LANES:] = lo
-
-    flip(x1, t1)
-    flip(x2, t2)
+            keep(b, x2[b])
 
     spot = jnp.where((lane == row + v_at) & (row < n), 1.0, 0.0)[:n]
 
@@ -332,32 +369,30 @@
         hi, lo = split(x)
         return dot(tile, hi) + dot(tile, lo)
 
-    def weights(x):
-        hi, lo = split(x.T[v_at:lo_at])
-        both = jnp.concatenate([hi, lo], axis=0)
-        return jnp.concatenate([both, both], axis=1)
+    def tall(x):
+        return jnp.concatenate(split(x), axis=0)
 
     def halves(r):
         return r[:n] + r[n:]
 
+    def across(x):
+        return x.T[v_at:lo_at]
+
     mine = pl.ds(pl.multiple_of(me * w, w), w)
 
-    def opening():
-        one = weights(near(states[0, mine], states[1, mine], True))
+    def opening(dst, src):
+        one = tall(across(near(states[0, mine], states[1, mine], True)))
+        for b in range(nb):
+            dst[:, b * bs : (b + 1) * bs] = halves(dot(one, src[b]))
+
+    def closing(last):
+        two = tall(last)
         for b in range(nb):
             at = slice(b * bs, (b + 1) * bs)
-            first[:, at] = halves(dot(one, t1[b]))
-            second[:, at] = halves(dot(one, t2[b]))
+            second[:, at] = second[:, at] + halves(dot(two, t1[b]))
 
     each(R - 1, lambda i: arrive(0, send0, got0, i))
     if R <= 8:
-        def sweep(wv, order):
-            s, out = zero, [None] * R
-            for i, d in enumerate(order):
-                out[d] = s
-                s = s + part(wv, i)
-            return out
-
         up, down = list(range(R)), list(range(R - 1, -1, -1))
         tiles = [got0[d] for d in range(R)]
         wide = [t.astype(f32) for t in tiles]
@@ -369,28 +404,78 @@
                 [jnp.where(inner, -pltpu.roll(wide[d], LANES - w, 1), 0.0) for d in down], w, out_b
             ),
         )
-        fwd, bwd = joined(out_f).astype(bf16), joined(out_b).astype(bf16)
-
-        def carry(m, inverse, order):
+        tiled = range(R // per)
+
+        def carry(m, out, order):
             u = jnp.concatenate([m[d] for d in order], axis=0)
-            return sweep(u + dot(inverse, u.astype(bf16)), order)
+            wv = u + dot(joined(out).astype(bf16), u.astype(bf16))
+            s, res = zero, [None] * R
+            for i, d in enumerate(order):
+                res[d] = s
+                s = s + part(wv, i)
+            return res
 
         mid = between(w, v_at, lo_at)
-        s1 = carry([jnp.where(mid, wide[d], 0.0) for d in up], fwd, up)
+        s1 = carry([jnp.where(mid, wide[d], 0.0) for d in up], out_f, up)
         m2 = [dot(tiles[d], late(s1[d], True).astype(bf16)) for d in up]
-        s2 = carry(m2, bwd, down)
+        s2 = carry(m2, out_b, down)
         for d in up:
             states[0, d * w : (d + 1) * w] = s1[d]
             states[1, d * w : (d + 1) * w] = s2[d]
-        opening()
+        g = [across(near(s1[d], s2[d], True)).astype(bf16) for d in up]
+
+        def reach(k, out, order):
+            s = [zero for _ in tiled]
+            for i, d in enumerate(order):
+                for t in tiled:
+                    maps[k, d * w : (d + 1) * w, t * LANES : (t + 1) * LANES] = s[t]
+                s = [s[t] + out[i][t] + home(i, t) for t in tiled]
+            return maps[k, mine]
+
+        own_f = reach(0, out_f, up)
+        own_b = reach(1, out_b, down)
+        whole_f = maps[0].astype(bf16)
+        gates = []
+        own_bt = own_b.T
+        for d in up:
+            i = R - 1 - d
+            gates.append(own_bt[i * w : (i + 1) * w])
+        across_rows = jnp.concatenate(
+            [
+                lax.dot_general(
+                    pltpu.roll(wide[d], w, 1).astype(bf16)[:, :w], gates[d].astype(bf16),
+                    (((0,), (0,)), ((), ())), preferred_element_type=f32,
+                )
+                for d in up
+            ],
+            axis=0,
+        )
+        joint_t = lax.dot_general(
+            whole_f, across_rows.astype(bf16), (((0,), (0,)), ((), ())), preferred_element_type=f32
+        )
+        own_ft = own_f.T
+        none = jnp.zeros((w, w), f32)
+        moves = []
+        for d in up:
+            at_d = slice(d * w, (d + 1) * w)
+            moves.append(
+                jnp.concatenate(
+                    [
+                        jnp.concatenate([own_ft[at_d], joint_t[at_d], none, none], axis=1),
+                        jnp.concatenate([none, gates[d], none, none], axis=1),
+                    ],
+                    axis=0,
+                ).astype(bf16)
+            )
+        opening(first, t1)
         each(R - 1, lambda i: arrive(1, send1, got1, i))
-        m34 = [dot(got1[d], near(s1[d], s2[d], True).astype(bf16)) for d in up]
-        s3 = carry([m34[d][:w] for d in up], fwd, up)
-        m4 = [m34[d][w:] + dot(tiles[d], late(s3[d], False).astype(bf16)) for d in up]
-        s4 = carry(m4, bwd, down)
+        heard = [dot_nt(g[d], got1[d]).astype(bf16) for d in up]
+        opening(second, t2)
+        last = None
         for d in up:
-            states[2, d * w : (d + 1) * w] = s3[d]
-            states[3, d * w : (d + 1) * w] = s4[d]
+            r = dot(heard[d], moves[d])
+            last = r if last is None else last + r
+        closing(last)
     else:
         def at(d):
             return pl.ds(pl.multiple_of(d * w, w), w)
@@ -412,7 +497,8 @@
 
         walk(0, lambda d, s: times(got0[d], ahead(s, True)), False)
         walk(1, lambda d, s: times(got0[d], late(states[0, at(d)], True, s)), True)
-        opening()
+        opening(first, t1)
+        opening(second, t2)
         each(R - 1, lambda i: arrive(1, send1, got1, i))
         walk(
             2,
@@ -425,14 +511,21 @@
             + times(got0[d], late(states[2, at(d)], False, s)),
             True,
         )
-
-    two = weights(near(states[2, mine], states[3, mine], False))
-    for b in range(nb):
-        at = slice(b * bs, (b + 1) * bs)
-        second[:, at] = second[:, at] + halves(dot(two, t1[b]))
+        closing(across(near(states[2, mine], states[3, mine], False)))
 
     each(R - 1, lambda i: copy(0, send0, got0, i).wait_send())
     each(R - 1, lambda i: copy(1, send1, got1, i).wait_send())
+
+
+def deliver(x, y, x_out, y_out, sem):
+    copies = [
+        pltpu.make_async_copy(src, dst, sem.at[i])
+        for i, (src, dst) in enumerate(((x, x_out), (y, y_out)))
+    ]
+    for cp in copies:
+        cp.start()
+    for cp in copies:
+        cp.wait()
 
 
 def local(R, rhs, linv, lleft, lright, uinv, uleft, uright, ranks):
@@ -445,7 +538,7 @@
     slim = pltpu.VMEM((nb, w, bs), bf16)
     tall = pltpu.VMEM((nb, bs, LANES), f32)
     args = (rhs, linv, flip(lleft), flip(lright), uinv, flip(uleft), flip(uright), ranks)
-    return pl.pallas_call(
+    results = pl.pallas_call(
         functools.partial(kernel, R, nb, bs, w, n),
         out_shape=(out, out),
         in_specs=[hbm] * 8,
@@ -454,17 +547,19 @@
             pltpu.VMEM(rhs.shape, bf16),
             slim, slim, slim, slim,
             pltpu.SMEM(ranks.shape, jnp.int32),
-            pltpu.VMEM((2, nb, bs + 3 * w, bs), bf16),
+            pltpu.VMEM((2, nb, bs + w, bs), bf16),
+            pltpu.VMEM((nb, 2 * w, bs), bf16),
             pltpu.VMEM((2, nb, bs, LANES), bf16),
             pltpu.VMEM((2, nb * w, nb * w), bf16),
             tall, tall, tall,
-            pltpu.VMEM((nb, 2 * LANES, bs), bf16),
-            pltpu.VMEM((nb, 2 * LANES, bs), bf16),
+            pltpu.VMEM((nb, LANES, bs), bf16),
+            pltpu.VMEM((nb, LANES, bs), bf16),
             pltpu.VMEM((w, LANES), bf16),
             pltpu.VMEM((2 * w, LANES), bf16),
             pltpu.VMEM((R, w, LANES), bf16),
             pltpu.VMEM((R, 2 * w, LANES), bf16),
             pltpu.VMEM((4, R * w, LANES), f32),
+            pltpu.VMEM((2, R * w, min(R, 8) * w), f32),
             pltpu.SemaphoreType.DMA((6,)),
             pltpu.SemaphoreType.DMA((2, nb)),
             pltpu.SemaphoreType.DMA((2, R)),
@@ -474,6 +569,14 @@
             collective_id=0, has_side_effects=True, vmem_limit_bytes=33554432
         ),
     )(*[pltpu.with_memory_space_constraint(a, pltpu.HBM) for a in args])
+    return pl.pallas_call(
+        deliver,
+        out_shape=(out, out),
+        in_specs=[pl.BlockSpec(memory_space=pl.ANY)] * 2,
+        out_specs=(hbm, hbm),
+        scratch_shapes=[pltpu.SemaphoreType.DMA((2,))],
+        compiler_params=pltpu.CompilerParams(vmem_limit_bytes=1048576),
+    )(*[pltpu.with_memory_space_constraint(r, pltpu.VMEM) for r in results])
 
 
 def solution(mesh):

time: 17.7 us -> 16.7 us (0.944)
  local copies, waits for them, and re-layouts: 1.31 us -> 0 us
  Pallas kernels: 15.6 us -> 15.9 us
    unnamed x2 -> x0, local copies, waits for them, and re-layouts: 1.31 us -> none
    pallas_call x0 -> x1, Pallas kernels: none -> 0.72 us  [local(): pl.pallas_call(deliver, out_shape=(out, out), in_specs=[pl.BlockSpec(memo...]
    pallas_call x1, Pallas kernels: 15.6 us -> 15.2 us  [local(): pl.pallas_call(functools.partial(kernel, R, nb, bs, w, n), out_shape=(out...]
where the time goes in v5:
time: 16.7 us; the launch traced here: 16.5 us
  Pallas kernels  15.9 us (95%)
  between operations  0.64 us (4%)
    pallas_call x1, Pallas kernels, local(): pl.pallas_call(functools.partial(kernel, R, nb, bs, w, n), out_shape=(out...  15.2 us
    pallas_call x1, Pallas kernels, local(): pl.pallas_call(deliver, out_shape=(out, out), in_specs=[pl.BlockSpec(memo...  0.72 us

profile of v5, /device:TPU:0, one launch (start us, length us, event | category | flops | bytes accessed | tf_op | source)
XLA Modules:
  0.0 16.5 jit_solution(3768100110755442758)
XLA Ops:
  0.6 15.2 %shard_map.95 = (f32[16,2048]{1,0:T(8,128)S(1)}, f32[16,2048]{1,0:T(8,128)S(1)}) custom-call(bf16[16,2048]{1,0:T(8,128)(2,1)} %rhs_h.1, bf16[8,256,256]{2,1,0:T(8,128)(2,1)} %linv_h.1, bf16[8,32,256]{2,1,0:T(8,128)(2,1)} %bitcast.4, bf16[8,32,256]{2,1,0:T(8,128)(2,1)} %bitcast.5, bf16[8,256,256]{2,1,0:T(8,128)(2,1)} %uinv_h.1, bf16[8,32,256]{2,1,0:T(8,128)(2,1)} %bitcast.6, ...), custom_call_target="tpu_custom_call" | custom-call | tf_op jit(solution)/shard_map/pallas_call | solution.py:541
  15.8 0.7 %shard_map.96 = (f32[16,2048]{1,0:T(8,128)}, f32[16,2048]{1,0:T(8,128)}) custom-call(f32[16,2048]{1,0:T(8,128)S(1)} %get-tuple-element.4.x, f32[16,2048]{1,0:T(8,128)S(1)} %get-tuple-element.5.y), custom_call_target="tpu_custom_call" | custom-call | tf_op jit(solution)/shard_map/pallas_call | solution.py:572

commit v6 on v5

--- a/solution.py
+++ b/solution.py
@@ -322,7 +322,8 @@
         ).wait_recv()
 
     pl.semaphore_wait(barrier, R - 1)
-    each(R - 1, lambda i: copy(0, send0, got0, i).start())
+    near_count = max(1, R // 4)
+    each(near_count, lambda i: copy(0, send0, got0, i).start())
     got0[me] = send0[...]
 
     solve(1, w_b + w_u, pushed, x1, eye_u)
@@ -331,7 +332,9 @@
         r = dot(adj[b], x1[b].astype(bf16))
         ends = r if ends is None else ends + r
     send1[...] = ends.astype(bf16)
-    each(R - 1, lambda i: copy(1, send1, got1, i).start())
+    each(near_count, lambda i: copy(1, send1, got1, i).start())
+    each(R - 1 - near_count, lambda i: copy(0, send0, got0, near_count + i).start())
+    each(R - 1 - near_count, lambda i: copy(1, send1, got1, near_count + i).start())
     got1[me] = send1[...]
 
     @pl.when(me >= 0)

time: 16.7 us -> 16.1 us (0.964)
  Pallas kernels: 15.9 us -> 15.3 us
    pallas_call x1, Pallas kernels: 15.2 us -> 14.6 us  [local(): pl.pallas_call(functools.partial(kernel, R, nb, bs, w, n), out_shape=(out...]
where the time goes in v6:
time: 16.1 us; the launch traced here: 15.9 us
  Pallas kernels  15.3 us (95%)
  between operations  0.64 us (4%)
    pallas_call x1, Pallas kernels, local(): pl.pallas_call(functools.partial(kernel, R, nb, bs, w, n), out_shape=(out...  14.6 us
    pallas_call x1, Pallas kernels, local(): pl.pallas_call(deliver, out_shape=(out, out), in_specs=[pl.BlockSpec(memo...  0.72 us

profile of v6, /device:TPU:0, one launch (start us, length us, event | category | flops | bytes accessed | tf_op | source)
XLA Modules:
  0.0 15.9 jit_solution(8891330908808935320)
XLA Ops:
  0.6 14.6 %shard_map.95 = (f32[16,2048]{1,0:T(8,128)S(1)}, f32[16,2048]{1,0:T(8,128)S(1)}) custom-call(bf16[16,2048]{1,0:T(8,128)(2,1)} %rhs_h.1, bf16[8,256,256]{2,1,0:T(8,128)(2,1)} %linv_h.1, bf16[8,32,256]{2,1,0:T(8,128)(2,1)} %bitcast.4, bf16[8,32,256]{2,1,0:T(8,128)(2,1)} %bitcast.5, bf16[8,256,256]{2,1,0:T(8,128)(2,1)} %uinv_h.1, bf16[8,32,256]{2,1,0:T(8,128)(2,1)} %bitcast.6, ...), custom_call_target="tpu_custom_call" | custom-call | tf_op jit(solution)/shard_map/pallas_call | solution.py:544
  15.2 0.7 %shard_map.96 = (f32[16,2048]{1,0:T(8,128)}, f32[16,2048]{1,0:T(8,128)}) custom-call(f32[16,2048]{1,0:T(8,128)S(1)} %get-tuple-element.4.x, f32[16,2048]{1,0:T(8,128)S(1)} %get-tuple-element.5.y), custom_call_target="tpu_custom_call" | custom-call | tf_op jit(solution)/shard_map/pallas_call | solution.py:575
